TPU v7x, 32 devices: a whole 2x2x4 slice. The times are simulated.
32 devices in a mesh: groups: 2 (over y), context: 8 (over z, x), tensor: 2 (over core).
Axes of the slice: x: 2, y: 2, z: 4, core: 2. Of those that a mesh axis runs over, the one named last changes fastest.
Arguments:
- self_queries: bfloat16 [1280, 2048], P(('groups', 'context'), 'tensor'), parts along dimension 0, may hold values from -512 to 512
- self_keys: bfloat16 [1280, 512], P(('groups', 'context'), 'tensor'), parts along dimension 0, may hold values from -6 to 6
- self_values: bfloat16 [1280, 512], P(('groups', 'context'), 'tensor'), parts along dimension 0, may hold values from -6 to 6
- cross_queries: bfloat16 [1280, 2048], P(('groups', 'context'), 'tensor'), parts along dimension 0, may hold values from -512 to 512
- cross_keys: bfloat16 [384, 512], P(('groups', 'context'), 'tensor'), parts along dimension 0, may hold values from -6 to 6
- cross_values: bfloat16 [384, 512], P(('groups', 'context'), 'tensor'), parts along dimension 0, may hold values from -6 to 6
- span_order: int32 [32], P('groups'), parts along dimension 0, may hold values from 0 to 15, as said below
Outputs:
- self_out: bfloat16 [1280, 2048], P(('groups', 'context'), 'tensor'), parts along dimension 0
- cross_out: bfloat16 [1280, 2048], P(('groups', 'context'), 'tensor'), parts along dimension 0
There are 2 independent parts, one for each index of `groups`. A program takes and returns all parts, laid end to end along the dimension named above; each array names one. Nothing has to cross between parts.
Inputs may be any that keep to these rules, and one draw needn't show every extreme that they name: `span_order`: each of 0 to 15 appears once, and entries 2 d and 2 d + 1 sum to 15.
All inputs are finite; a program needn't handle non-finite values.
Results may differ from a plain program's by a relative error of at most 0.012.
The roundings to bfloat16 on the way count: a program that leaves them out, or rounds other values in their place, can miss the bound.
Values may be sent and summed in bfloat16 or wider, within the bound.
A program may use at most 128 MiB of HBM per device.

v0:
```python
import jax
import jax.numpy as jnp
from jax import lax
from jax.sharding import PartitionSpec as P

HEAD_DIM = 128
HEADS = 16
KV_HEADS = 4


NEG_FILL = -1e30


def rotary(values, places):
    half_dim = values.shape[-1] // 2
    frequency = 500000.0 ** (-(jnp.arange(half_dim, dtype=jnp.float32) * 2.0) / values.shape[-1])
    angles = places.astype(jnp.float32)[:, None] * frequency[None, :]
    cosine = jnp.cos(angles)[:, None, :]
    sine_part = jnp.sin(angles)[:, None, :]
    first_half = values[..., :half_dim]
    second_half = values[..., half_dim:]
    return jnp.concatenate(
        [
            first_half * cosine - second_half * sine_part,
            second_half * cosine + first_half * sine_part,
        ],
        -1,
    )


def update_rows(carry_state, queries, query_places, key_rows, value_rows, key_places):
    row_peak, weight_sum, mixed_sum = carry_state
    scores = jnp.einsum(
        "qkgd,rkd->kgqr", queries, key_rows, preferred_element_type=jnp.float32
    ) * queries.shape[-1] ** (-0.5)
    if key_places is not None:
        allowed = (key_places[None, :] <= query_places[:, None])[None, None]
        scores = jnp.where(allowed, scores, NEG_FILL)
    new_peak = jnp.maximum(row_peak, jnp.max(scores, -1))
    weights = jnp.exp(scores - new_peak[..., None])
    if key_places is not None:
        weights = jnp.where(allowed, weights, 0.0)
    factor = jnp.exp(row_peak - new_peak)
    weight_sum = weight_sum * factor + jnp.sum(weights, -1)
    mixed_sum = mixed_sum * factor[..., None] + jnp.einsum(
        "kgqr,rkd->kgqd",
        weights.astype(jnp.bfloat16),
        value_rows,
        preferred_element_type=jnp.float32,
    )
    return (new_peak, weight_sum, mixed_sum)


def advance(carry_state, queries, query_places, key_rows, value_rows, key_places):
    if key_places is None:
        return update_rows(carry_state, queries, query_places, key_rows, value_rows, None)
    return update_rows(carry_state, queries, query_places, key_rows, value_rows, key_places)


def sweep_keys(carry_state, queries, query_places, key_rows, value_rows, key_places):
    row_total = key_rows.shape[0]
    block_rows = row_total
    while block_rows > 512 and block_rows % 2 == 0:
        block_rows = block_rows // 2
    if block_rows == row_total:
        return advance(carry_state, queries, query_places, key_rows, value_rows, key_places)
    block_count = row_total // block_rows
    key_blocks = key_rows.reshape((block_count, block_rows) + key_rows.shape[1:])
    value_blocks = value_rows.reshape((block_count, block_rows) + value_rows.shape[1:])
    if key_places is None:

        def plain_step(inner_state, arrived):
            return (advance(inner_state, queries, query_places, arrived[0], arrived[1], None), None)

        final_state, unused = lax.scan(plain_step, carry_state, (key_blocks, value_blocks))
    else:
        place_blocks = key_places.reshape(block_count, block_rows)

        def masked_step(inner_state, arrived):
            return (
                advance(inner_state, queries, query_places, arrived[0], arrived[1], arrived[2]),
                None,
            )

        final_state, unused = lax.scan(
            masked_step, carry_state, (key_blocks, value_blocks, place_blocks)
        )
    return final_state


def finish(carry_state):
    row_peak, weight_sum, mixed_sum = carry_state
    result = mixed_sum / weight_sum[..., None]
    result = jnp.transpose(result, (2, 0, 1, 3))
    return result.reshape(result.shape[0], -1).astype(jnp.bfloat16)


def body(self_queries, self_keys, self_values, cross_queries, cross_keys, cross_values, span_order):
    local_rows = self_queries.shape[0]
    span_len = local_rows // 2
    kv_local = self_keys.shape[1] // HEAD_DIM
    group_size = HEADS // KV_HEADS
    device = lax.axis_index("context")
    owned_spans = lax.dynamic_slice(span_order, (2 * device,), (2,))
    within_span = jnp.arange(span_len, dtype=jnp.int32)[None, :]
    query_places = (owned_spans[:, None] * span_len + within_span).reshape(-1)
    text_queries = rotary(
        self_queries.astype(jnp.float32).reshape(local_rows, kv_local * group_size, HEAD_DIM),
        query_places,
    )
    text_queries = text_queries.astype(jnp.bfloat16).reshape(
        local_rows, kv_local, group_size, HEAD_DIM
    )
    text_keys = rotary(
        self_keys.astype(jnp.float32).reshape(local_rows, kv_local, HEAD_DIM), query_places
    )
    text_keys = text_keys.astype(jnp.bfloat16).reshape(local_rows, kv_local * HEAD_DIM)
    image_queries = cross_queries.reshape(local_rows, kv_local, group_size, HEAD_DIM)
    empty_state = (
        jnp.full((kv_local, group_size, local_rows), NEG_FILL, jnp.float32),
        jnp.zeros((kv_local, group_size, local_rows), jnp.float32),
        jnp.zeros((kv_local, group_size, local_rows, HEAD_DIM), jnp.float32),
    )
    piece_keys = lax.all_gather(text_keys, "context", axis=0, tiled=True)
    piece_values = lax.all_gather(self_values, "context", axis=0, tiled=True)
    piece_rows = piece_keys.shape[0]
    key_places = (span_order[:, None] * span_len + within_span).reshape(-1)
    self_state = sweep_keys(
        empty_state,
        text_queries,
        query_places,
        piece_keys.reshape(piece_rows, kv_local, HEAD_DIM),
        piece_values.reshape(piece_rows, kv_local, HEAD_DIM),
        key_places,
    )
    piece_keys = lax.all_gather(cross_keys, "context", axis=0, tiled=True)
    piece_values = lax.all_gather(cross_values, "context", axis=0, tiled=True)
    piece_rows = piece_keys.shape[0]
    cross_state = sweep_keys(
        empty_state,
        image_queries,
        None,
        piece_keys.reshape(piece_rows, kv_local, HEAD_DIM),
        piece_values.reshape(piece_rows, kv_local, HEAD_DIM),
        None,
    )
    return (finish(self_state), finish(cross_state))


def solution(mesh):
    in_specs = (
        P(("groups", "context"), "tensor"),
        P(("groups", "context"), "tensor"),
        P(("groups", "context"), "tensor"),
        P(("groups", "context"), "tensor"),
        P(("groups", "context"), "tensor"),
        P(("groups", "context"), "tensor"),
        P("groups"),
    )
    out_specs = (P(("groups", "context"), "tensor"), P(("groups", "context"), "tensor"))
    return jax.shard_map(body, mesh=mesh, in_specs=in_specs, out_specs=out_specs, check_vma=False)
```

profile of v0, /device:TPU:0, one launch (start us, length us, event | category | flops | bytes accessed | tf_op | source)
XLA Modules:
  0.0 137.6 jit_solution(15886606267143810849)
XLA Ops:
  0.6 0.0 copy-start.5
  0.6 0.6 copy-done.5
  1.3 0.1 dynamic-slice_multiply_fusion
  1.4 0.1 add_convert_fusion.2
  1.4 0.1 convert_element_type.42
  1.5 0.2 multiply_cosine_fusion
  1.8 0.9 convert_bitcast_fusion
  2.7 0.1 copy.35
  2.8 0.2 fusion.25
  2.9 0.1 subtract_convert_fusion
  3.1 0.0 copy-start.1
  3.1 0.1 pad_maximum_fusion
  3.2 0.6 copy-done.1
  3.9 0.2 subtract_convert_fusion.1
  4.1 0.1 pad_maximum_fusion.1
  4.3 32.7 %all_gather.12 = bf16[640,256]{1,0:T(8,128)(2,1)S(1)} all-gather(bf16[80,256]{1,0:T(8,128)(2,1)S(1)} %bitcast.59), channel_id=1, replica_groups=mesh['groups'=2,'context'=8,'tensor'=2] {'context'}, dimensions={0}, use_global_device_ids=true | all-gather | bytes 368640 | tf_op jit(solution)/shard_map/all_gather | solution.py:124
  36.9 0.0 copy-start.2
  36.9 0.1 reshape_reshape.7
  37.0 0.7 copy-done.2
  37.7 30.8 %all_gather.13 = bf16[640,256]{1,0:T(8,128)(2,1)S(1)} all-gather(bf16[80,256]{1,0:T(8,128)(2,1)S(1)} %copy-done.2), channel_id=1, replica_groups=mesh['groups'=2,'context'=8,'tensor'=2] {'context'}, dimensions={0}, use_global_device_ids=true | all-gather | bytes 368640 | tf_op jit(solution)/shard_map/all_gather | solution.py:125
  68.5 0.1 reshape_reshape.8
  68.6 0.1 add.71
  68.7 0.1 add.72
  68.8 0.1 add.73
  68.9 0.1 add.75
  69.0 3.6 %while.15 = (s32[]{:T(128)}, f32[2,4,80]{2,1,0:T(4,128)S(1)}, f32[2,4,80]{2,1,0:T(4,128)S(1)}, f32[2,4,80,128]{3,2,1,0:T(8,128)S(1)}, s32[2,320]{1,0:T(2,128)S(1...) while((s32[]{:T(128)}, f32[2,4,80]{2,1,0:T(4,128)S(1)}, ...), condition=%wide.region_3.4_spmd.clone, body=%wide.region_0.3_spmd.clone.sunk | while | flops 106975440 | bytes 4408457 | solution.py:85
  69.0 0.1 iota_add_fusion.2
  69.1 0.1 le.33
  69.2 0.1 broadcast_compare_fusion.2
  69.3 0.2 constant_dynamic-slice_fusion.3
  69.5 0.4 fusion.35
  70.0 0.4 fusion.36
  70.4 0.4 convolution_add_fusion.2
  70.8 0.1 iota_add_fusion.2
  70.9 0.1 le.33
  71.0 0.1 broadcast_compare_fusion.2
  71.1 0.2 constant_dynamic-slice_fusion.3
  71.3 0.4 fusion.35
  71.7 0.4 fusion.36
  72.2 0.4 convolution_add_fusion.2
  72.6 0.2 fusion.21
  72.7 0.1 copy.17
  72.8 0.0 copy-start.3
  72.8 0.8 convert_element_type.46
  73.6 0.0 copy-done.3
  73.6 0.0 copy-start
  73.6 30.7 %all_gather.14 = bf16[192,256]{1,0:T(8,128)(2,1)S(1)} all-gather(bf16[24,256]{1,0:T(8,128)(2,1)S(1)} %copy-done.3), channel_id=1, replica_groups=mesh['groups'=2,'context'=8,'tensor'=2] {'context'}, dimensions={0}, use_global_device_ids=true | all-gather | bytes 110592 | tf_op jit(solution)/shard_map/all_gather | solution.py:136
  104.3 0.0 copy-done
  104.3 0.1 reshape.166
  104.4 0.4 fusion.26
  104.8 0.4 fusion.16
  105.2 0.0 copy-start.4
  105.2 0.7 copy-done.4
  105.9 30.5 %all_gather.15 = bf16[192,256]{1,0:T(8,128)(2,1)S(1)} all-gather(bf16[24,256]{1,0:T(8,128)(2,1)S(1)} %copy-done.4), channel_id=1, replica_groups=mesh['groups'=2,'context'=8,'tensor'=2] {'context'}, dimensions={0}, use_global_device_ids=true | all-gather | bytes 110592 | tf_op jit(solution)/shard_map/all_gather | solution.py:137
  136.5 0.3 fusion.15
  136.8 0.1 copy.21
  136.9 0.8 convert_element_type.49
  (21 shorter events, 0.3 us)
Async XLA Ops:
  0.6 0.7 copy-start.5
  3.1 0.8 copy-start.1
  36.9 0.8 copy-start.2
  72.8 0.8 copy-start.3
  73.6 30.7 %copy-start = (bf16[80,1024]{1,0:T(8,128)(2,1)S(1)}, bf16[80,1024]{1,0:T(8,128)(2,1)}, u32[]{:S(2)}) copy-start(bf16[80,1024]{1,0:T(8,128)(2,1)} %param.12) | copy-start | bytes 491524
  105.2 0.7 copy-start.4
where the time goes:
time: 138 us
  blocking collectives  125 us (91%)
  local copies, waits for them, and re-layouts  6.03 us (4%)
  other arithmetic  3.61 us (3%)
  matrix products  2.35 us (2%)
    all_gather x1, blocking collectives, body(): piece_keys = lax.all_gather(text_keys, 'context', axis=0, tiled=True)  32.7 us
    all_gather x1, blocking collectives, body(): piece_values = lax.all_gather(self_values, 'context', axis=0, tiled=True)  30.8 us
    all_gather x1, blocking collectives, body(): piece_keys = lax.all_gather(cross_keys, 'context', axis=0, tiled=True)  30.7 us
    all_gather x1, blocking collectives, body(): piece_values = lax.all_gather(cross_values, 'context', axis=0, tiled=True)  30.5 us
    unnamed x14, local copies, waits for them, and re-layouts  2.76 us

commit v1 on v0

v1 whole, which is shorter than its diff:
```python
import functools
import math

import jax
import jax.numpy as jnp
import numpy as np
from jax import lax
from jax.experimental import pallas as pl
from jax.experimental.pallas import tpu as pltpu
from jax.sharding import PartitionSpec as P

HEAD_DIM = 128
HEADS = 16
KV_HEADS = 4
GROUP = HEADS // KV_HEADS
NEG_FILL = -1e30
SCALE = HEAD_DIM ** (-0.5) * math.log2(math.e)
UP, DOWN, RIGHT, LEFT = range(4)


def rotary_tables(spans, span_len):
    half = HEAD_DIM // 2
    frequency = 500000.0 ** (-(np.arange(half) * 2.0) / HEAD_DIM)
    frequency = np.concatenate([frequency, frequency])
    base = (np.arange(spans) * span_len)[:, None] * frequency[None, :]
    inner = np.arange(span_len)[:, None] * frequency[None, :]
    sign = np.where(np.arange(HEAD_DIM) < half, -1.0, 1.0)[None, :]
    bases = np.stack([np.cos(base), np.sin(base)])
    inners = np.stack([np.cos(inner), np.sin(inner), np.cos(inner) * sign, np.sin(inner) * sign])
    return bases.astype(np.float32), inners.astype(np.float32)


def for_range(low, high, step):
    if high - low <= 4:
        for index in range(low, high):
            step(index)
    else:
        lax.fori_loop(low, high, lambda index, unused: (step(index), 0)[1], 0)


def is_zero(distance):
    return isinstance(distance, int) and distance == 0


def kernel(
    n, nx,
    order, q_hbm, k_hbm, v_hbm, cq_hbm, ck_hbm, cv_hbm, bases_hbm, inners_hbm,
    out_hbm, cout_hbm,
    text, image, q_in, cq_in, bases, inners, q_rot, peak, total, mixed, out_v, cout_v,
    load_sem, out_sem, text_send, text_recv, image_send, image_recv,
):
    nz = n // nx
    me = lax.axis_index("context")
    z, x = me // nx, lax.rem(me, nx)
    rows = q_in.shape[0]
    span_len = rows // 2
    kv_local = text.shape[3] // HEAD_DIM
    image_rows = image.shape[2]

    exists = (z < nz - 1, z > 0, x < nx - 1, x > 0)
    neighbour = (me + nx, me - nx, me + 1, me - 1)

    kv_loads = [
        pltpu.make_async_copy(k_hbm, text.at[me, 0], load_sem.at[0]),
        pltpu.make_async_copy(v_hbm, text.at[me, 1], load_sem.at[1]),
        pltpu.make_async_copy(ck_hbm, image.at[me, 0], load_sem.at[2]),
        pltpu.make_async_copy(cv_hbm, image.at[me, 1], load_sem.at[3]),
    ]
    other_loads = [
        pltpu.make_async_copy(bases_hbm, bases, load_sem.at[4]),
        pltpu.make_async_copy(inners_hbm, inners, load_sem.at[5]),
        pltpu.make_async_copy(q_hbm, q_in, load_sem.at[6]),
        pltpu.make_async_copy(cq_hbm, cq_in, load_sem.at[7]),
    ]
    for load in kv_loads + other_loads:
        load.start()

    barrier = pltpu.get_barrier_semaphore()
    for way in range(4):
        @pl.when(exists[way])
        def _():
            pl.semaphore_signal(
                barrier, inc=1, device_id={"context": neighbour[way]},
                device_id_type=pl.DeviceIdType.MESH,
            )
    pl.semaphore_wait(barrier, sum(e.astype(jnp.int32) for e in exists))
    for load in kv_loads:
        load.wait()

    def text_copy(slot, part, way):
        return pltpu.make_async_remote_copy(
            src_ref=text.at[slot, part], dst_ref=text.at[slot, part],
            send_sem=text_send.at[slot, part, way], recv_sem=text_recv.at[slot, part],
            device_id={"context": neighbour[way]}, device_id_type=pl.DeviceIdType.MESH,
        )

    def image_copy(slot, way):
        return pltpu.make_async_remote_copy(
            src_ref=image.at[slot], dst_ref=image.at[slot],
            send_sem=image_send.at[slot, way], recv_sem=image_recv.at[slot],
            device_id={"context": neighbour[way]}, device_id_type=pl.DeviceIdType.MESH,
        )

    def ways_of(rel_first, rel_second, first, second):
        ways = []
        if rel_second == 0:
            if rel_first <= 0:
                ways.append(first[0])
            if rel_first >= 0:
                ways.append(first[1])
            ways += list(second)
        else:
            ways.append(second[0] if rel_second < 0 else second[1])
        return ways

    def place(rel, distance, own, count):
        at = own + rel * distance
        valid = True if rel == 0 else (at >= 0 if rel < 0 else at < count)
        return at, valid

    def visit(rel_z, dz, rel_x, dx, action):
        at_z, valid_z = place(rel_z, dz, z, nz)
        at_x, valid_x = place(rel_x, dx, x, nx)
        slot = at_z * nx + at_x
        if rel_z == 0 and rel_x == 0:
            action(slot)
            return
        valid = valid_z if rel_x == 0 else (valid_x if rel_z == 0 else jnp.logical_and(valid_z, valid_x))
        pl.when(valid)(lambda: action(slot))

    def send_text(slot, part, rel_z, rel_x, op):
        for way in ways_of(rel_z, rel_x, (UP, DOWN), (RIGHT, LEFT)):
            pl.when(exists[way])(lambda way=way: getattr(text_copy(slot, part, way), op)())

    def send_image(slot, rel_z, rel_x, op):
        for way in ways_of(rel_x, rel_z, (RIGHT, LEFT), (UP, DOWN)):
            pl.when(exists[way])(lambda way=way: getattr(image_copy(slot, way), op)())

    def relay_text(rel_z, dz, rel_x, dx):
        def action(slot):
            for part in range(2):
                text_copy(slot, part, UP).wait_recv()
                send_text(slot, part, rel_z, rel_x, "start")
        visit(rel_z, dz, rel_x, dx, action)

    def relay_image(rel_z, dz, rel_x, dx):
        def action(slot):
            image_copy(slot, UP).wait_recv()
            send_image(slot, rel_z, rel_x, "start")
        visit(rel_z, dz, rel_x, dx, action)

    send_text(me, 0, 0, 0, "start")
    send_text(me, 1, 0, 0, "start")
    send_image(me, 0, 0, "start")

    for load in other_loads:
        load.wait()

    def angles(slot):
        cosines, sines, starts = [], [], []
        for part in range(2):
            span = order[2 * slot + part]
            base_cos = bases[0, pl.ds(span, 1), :]
            base_sin = bases[1, pl.ds(span, 1), :]
            cosines.append(base_cos * inners[0] - base_sin * inners[1])
            sines.append(base_sin * inners[2] + base_cos * inners[3])
            starts.append(span * span_len)
        return jnp.concatenate(cosines, 0), jnp.concatenate(sines, 0), starts

    def rotate(values, cosine, sine):
        values = values.astype(jnp.float32)
        turned = pltpu.roll(values, HEAD_DIM // 2, 1)
        return (values * cosine + turned * sine).astype(jnp.bfloat16)

    def positions(starts, shape, axis):
        index = lax.broadcasted_iota(jnp.int32, shape, axis)
        return jnp.where(index < span_len, starts[0] + index, starts[1] + index - span_len)

    own_cos, own_sin, own_starts = angles(me)
    for head in range(kv_local * GROUP):
        q_rot[head // GROUP, pl.ds(head % GROUP * rows, rows), :] = rotate(
            q_in[:, head * HEAD_DIM:(head + 1) * HEAD_DIM], own_cos, own_sin)

    def dot_nt(a, b):
        return lax.dot_general(a, b, (((1,), (1,)), ((), ())), preferred_element_type=jnp.float32)

    def block(slot, first):
        cosine, sine, starts = angles(slot)
        allowed = positions(starts, (rows, rows), 1) <= positions(own_starts, (rows, rows), 0)
        for head in range(kv_local):
            columns = slice(head * HEAD_DIM, (head + 1) * HEAD_DIM)
            keys = rotate(text[slot, 0, :, columns], cosine, sine)
            scores = dot_nt(q_rot[head], keys) * SCALE
            scores = jnp.where(allowed[None], scores.reshape(GROUP, rows, rows), NEG_FILL)
            scores = scores.reshape(GROUP * rows, rows)
            top = jnp.max(scores, -1, keepdims=True)
            if not first:
                old = peak[head]
                top = jnp.maximum(top, old)
            weights = jnp.exp2(scores - top)
            summed = jnp.sum(weights, -1, keepdims=True)
            product = jnp.dot(
                weights.astype(jnp.bfloat16), text[slot, 1, :, columns],
                preferred_element_type=jnp.float32)
            if not first:
                factor = jnp.exp2(old - top)
                summed = summed + total[head] * factor
                product = product + mixed[head] * factor
            peak[head] = top
            total[head] = summed
            mixed[head] = product

    def blocks_at(dz, columns_of):
        count_x, at_x = columns_of
        low = (z - dz >= 0).astype(jnp.int32)
        high = (z + dz < nz).astype(jnp.int32)
        count = low + high if not is_zero(dz) else 1

        def step(index, unused):
            side, column = index // count_x, lax.rem(index, count_x)
            at_z = jnp.where(jnp.logical_and(side == 0, low == 1), z - dz, z + dz)
            block(at_z * nx + at_x(column), False)
            return 0

        lax.fori_loop(0, count * count_x, step, 0)

    own_column = (1, lambda column: x)
    other_columns = (nx - 1, lambda column: lax.rem(x + 1 + column, nx))

    block(me, True)

    sides = (-1, 1)

    def across_image(rel_z, dz):
        if rel_z != 0:
            relay_image(rel_z, dz, 0, 0)
        for rel_x in sides:
            for_range(1, nx, lambda dx: relay_image(rel_z, dz, rel_x, dx))

    def across_text(dz):
        for rel_z in ((0,) if is_zero(dz) else sides):
            for rel_x in sides:
                for_range(1, nx, lambda dx: relay_text(rel_z, dz, rel_x, dx))

    across_image(0, 0)

    def stage(dz, before):
        for rel_z in sides:
            relay_text(rel_z, dz, 0, 0)
        for rel_z in sides:
            across_image(rel_z, dz)
        if nx > 1:
            across_text(before)
            blocks_at(before, other_columns)
        blocks_at(dz, own_column)

    if nz > 1:
        stage(1, 0)
        for_range(2, nz, lambda dz: stage(dz, dz - 1))

    keys_all = image[:, 0].astype(jnp.float32).reshape(n * image_rows, -1).astype(jnp.bfloat16)
    values_all = image[:, 1].astype(jnp.float32).reshape(n * image_rows, -1).astype(jnp.bfloat16)
    for head in range(kv_local):
        columns = slice(head * HEAD_DIM, (head + 1) * HEAD_DIM)
        first_head = head * GROUP
        queries = jnp.concatenate(
            [cq_in[:, (first_head + g) * HEAD_DIM:(first_head + g + 1) * HEAD_DIM] for g in range(GROUP)], 0)
        scores = dot_nt(queries, keys_all[:, columns]) * SCALE
        weights = jnp.exp2(scores - jnp.max(scores, -1, keepdims=True))
        summed = jnp.sum(weights, -1, keepdims=True)
        product = jnp.dot(
            weights.astype(jnp.bfloat16), values_all[:, columns], preferred_element_type=jnp.float32)
        result = (product / summed).astype(jnp.bfloat16)
        for g in range(GROUP):
            cout_v[:, (first_head + g) * HEAD_DIM:(first_head + g + 1) * HEAD_DIM] = result[g * rows:(g + 1) * rows]
    cross_store = pltpu.make_async_copy(cout_v, cout_hbm, out_sem.at[0])
    cross_store.start()

    if nx > 1:
        last = nz - 1
        across_text(last)
        blocks_at(last, other_columns)

    for head in range(kv_local):
        result = (mixed[head] / total[head]).astype(jnp.bfloat16)
        for g in range(GROUP):
            at = head * GROUP + g
            out_v[:, at * HEAD_DIM:(at + 1) * HEAD_DIM] = result[g * rows:(g + 1) * rows]
    self_store = pltpu.make_async_copy(out_v, out_hbm, out_sem.at[1])
    self_store.start()

    def drain(rel_z, dz, rel_x, dx):
        def action(slot):
            for part in range(2):
                send_text(slot, part, rel_z, rel_x, "wait_send")
            send_image(slot, rel_z, rel_x, "wait_send")
        visit(rel_z, dz, rel_x, dx, action)

    def drain_row(rel_z, dz):
        drain(rel_z, dz, 0, 0)
        for rel_x in sides:
            for_range(1, nx, lambda dx: drain(rel_z, dz, rel_x, dx))

    drain_row(0, 0)
    for rel_z in sides:
        for_range(1, nz, lambda dz: drain_row(rel_z, dz))
    cross_store.wait()
    self_store.wait()


def body(n, nx, self_queries, self_keys, self_values, cross_queries, cross_keys, cross_values, span_order):
    rows, width = self_queries.shape
    kv_width = self_keys.shape[1]
    kv_local = kv_width // HEAD_DIM
    image_rows = cross_keys.shape[0]
    bases, inners = rotary_tables(span_order.shape[0], rows // 2)
    anywhere = pl.BlockSpec(memory_space=pl.ANY)
    result = jax.ShapeDtypeStruct((rows, width), jnp.bfloat16)
    return pl.pallas_call(
        functools.partial(kernel, n, nx),
        out_shape=(result, result),
        in_specs=[pl.BlockSpec(memory_space=pltpu.SMEM)] + [anywhere] * 8,
        out_specs=(anywhere, anywhere),
        scratch_shapes=[
            pltpu.VMEM((n, 2, rows, kv_width), jnp.bfloat16),
            pltpu.VMEM((n, 2, image_rows, kv_width), jnp.bfloat16),
            pltpu.VMEM((rows, width), jnp.bfloat16),
            pltpu.VMEM((rows, width), jnp.bfloat16),
            pltpu.VMEM(bases.shape, jnp.float32),
            pltpu.VMEM(inners.shape, jnp.float32),
            pltpu.VMEM((kv_local, GROUP * rows, HEAD_DIM), jnp.bfloat16),
            pltpu.VMEM((kv_local, GROUP * rows, 1), jnp.float32),
            pltpu.VMEM((kv_local, GROUP * rows, 1), jnp.float32),
            pltpu.VMEM((kv_local, GROUP * rows, HEAD_DIM), jnp.float32),
            pltpu.VMEM((rows, width), jnp.bfloat16),
            pltpu.VMEM((rows, width), jnp.bfloat16),
            pltpu.SemaphoreType.DMA((8,)),
            pltpu.SemaphoreType.DMA((2,)),
            pltpu.SemaphoreType.DMA((n, 2, 4)),
            pltpu.SemaphoreType.DMA((n, 2)),
            pltpu.SemaphoreType.DMA((n, 4)),
            pltpu.SemaphoreType.DMA((n,)),
        ],
        compiler_params=pltpu.CompilerParams(collective_id=0, has_side_effects=True),
    )(span_order, self_queries, self_keys, self_values, cross_queries, cross_keys, cross_values, bases, inners)


def fast_axis(mesh, n):
    line = mesh.devices[0, :, 0]
    coords = [getattr(device, "coords", None) for device in line]
    if any(c is None for c in coords):
        return 1
    nx = len({c[0] for c in coords})
    return nx if n % nx == 0 else 1


def solution(mesh):
    n = mesh.shape["context"]
    both = P(("groups", "context"), "tensor")
    return jax.shard_map(
        functools.partial(body, n, fast_axis(mesh, n)), mesh=mesh,
        in_specs=(both,) * 6 + (P("groups"),), out_specs=(both, both), check_vma=False)
```

time: 138 us -> 27 us (0.20)
  blocking collectives: 125 us -> 0 us
  Pallas kernels: 0 us -> 23.9 us
  local copies, waits for them, and re-layouts: 6.03 us -> 2.3 us
  other arithmetic: 3.61 us -> 0 us
  matrix products: 2.35 us -> 0 us
    all_gather x4 -> x0, blocking collectives: 125 us -> none  [the longest x1 32.7 us: body(): piece_keys = lax.all_gather(text_keys, 'context', axis=0, tiled=True)]
    pallas_call x0 -> x1, Pallas kernels: none -> 23.9 us  [body(): pl.pallas_call(functools.partial(kernel, n, nx), out_shape=(result, resul...]
    dot_general x6 -> x0, matrix products: 2.35 us -> none  [the longest x3 1.25 us: update_rows(): jnp.einsum('qkgd,rkd->kgqr', queries, key_rows, preferred_element_type=jn...]
    convert_element_type x5 -> x0, local copies, waits for them, and re-layouts: 1.74 us -> none  [the longest x4 1.65 us: finish(): return result.reshape(result.shape[0], -1).astype(jnp.bfloat16)]
    unnamed x14 -> x4, local copies, waits for them, and re-layouts: 2.76 us -> 2.3 us
where the time goes in v1:
time: 27 us; the launch traced here: 26.9 us
  Pallas kernels  23.9 us (89%)
  local copies, waits for them, and re-layouts  2.3 us (9%)
  between operations  0.65 us (2%)
    pallas_call x1, Pallas kernels, body(): pl.pallas_call(functools.partial(kernel, n, nx), out_shape=(result, resul...  23.9 us
    unnamed x4, local copies, waits for them, and re-layouts  2.3 us

profile of v1, /device:TPU:0, one launch (start us, length us, event | category | flops | bytes accessed | tf_op | source)
XLA Modules:
  0.0 26.9 jit_solution(8773563235507792481)
XLA Ops:
  0.6 23.9 %shard_map.104 = (bf16[80,1024]{1,0:T(8,128)(2,1)}, bf16[80,1024]{1,0:T(8,128)(2,1)}) custom-call(s32[16]{0:T(128)} %order.1, bf16[80,1024]{1,0:T(8,128)(2,1)} %q_hbm.1, bf16[80,256]{1,0:T(8,128)(2,1)} %k_hbm.1, bf16[80,256]{1,0:T(8,128)(2,1)} %v_hbm.1, bf16[80,1024]{1,0:T(8,128)(2,1)} %cq_hbm.1, bf16[24,256]{1,0:T(8,128)(2,1)} %ck_hbm.1, ...), custom_call_target="tpu_custom_call" | custom-call | tf_op jit(solution)/shard_map/pallas_call | solution.py:319
  24.6 0.0 copy-start
  24.6 1.6 %copy.13 = bf16[80,1024]{1,0:T(8,128)(2,1)} copy(bf16[80,1024]{1,0:T(8,128)(2,1)} %get-tuple-element.4) | data formatting | bytes 327680
  26.2 0.0 copy-done
  26.2 0.7 %copy.14 = bf16[80,1024]{1,0:T(8,128)(2,1)} copy(bf16[80,1024]{1,0:T(8,128)(2,1)S(1)} %copy-done) | data formatting | bytes 327680
Async XLA Ops:
  24.6 1.6 %copy-start = (bf16[80,1024]{1,0:T(8,128)(2,1)S(1)}, bf16[80,1024]{1,0:T(8,128)(2,1)}, u32[]{:S(2)}) copy-start(bf16[80,1024]{1,0:T(8,128)(2,1)} %get-tuple-element.5) | copy-start | bytes 491524

commit v2 on v1

v2 whole, which is shorter than its diff:
```python
import functools
import math

import jax
import jax.numpy as jnp
import numpy as np
from jax import lax
from jax.experimental import pallas as pl
from jax.experimental.pallas import tpu as pltpu
from jax.sharding import PartitionSpec as P

HEAD_DIM = 128
HEADS = 16
KV_HEADS = 4
GROUP = HEADS // KV_HEADS
NEG_FILL = -1e30
SCALE = HEAD_DIM ** (-0.5) * math.log2(math.e)


def rotary_tables(spans, span_len):
    half = HEAD_DIM // 2
    frequency = 500000.0 ** (-(np.arange(half) * 2.0) / HEAD_DIM)
    frequency = np.concatenate([frequency, frequency])
    base = (np.arange(spans) * span_len)[:, None] * frequency[None, :]
    inner = np.arange(span_len)[:, None] * frequency[None, :]
    sign = np.where(np.arange(HEAD_DIM) < half, -1.0, 1.0)[None, :]
    bases = np.stack([np.cos(base), np.sin(base)])
    inners = np.stack([np.cos(inner), np.sin(inner), np.cos(inner) * sign, np.sin(inner) * sign])
    return bases.astype(np.float32), inners.astype(np.float32)


def doubling(order):
    held, steps = [0], []
    for mask in order:
        steps.append((mask, list(held)))
        held += [item ^ mask for item in held]
    return steps


def kernel(
    n, nx,
    order, q_hbm, k_hbm, v_hbm, cq_hbm, ck_hbm, cv_hbm, bases_hbm, inners_hbm,
    out_v, cout_v,
    text, image, q_in, cq_in, bases, inners, q_rot, peak, total, mixed,
    load_sem, text_send, text_recv, image_send, image_recv,
):
    me = lax.axis_index("context")
    rows = q_in.shape[0]
    span_len = rows // 2
    kv_local = text.shape[3] // HEAD_DIM
    image_rows = image.shape[2]

    x_masks = [1 << b for b in reversed(range(nx.bit_length() - 1))]
    z_masks = [nx << b for b in reversed(range((n // nx).bit_length() - 1))]
    masks = z_masks + x_masks
    text_steps = doubling(z_masks + x_masks)
    image_steps = doubling(z_masks[:1] + x_masks + z_masks[1:])

    def flipped(index, item):
        for mask in masks:
            bit = (item // mask) % 2
            index = index + mask * bit * (1 - 2 * ((index // mask) % 2))
        return index

    partner = {mask: flipped(me, mask) for mask in masks}

    kv_loads = [
        pltpu.make_async_copy(k_hbm, text.at[0, 0], load_sem.at[0]),
        pltpu.make_async_copy(v_hbm, text.at[0, 1], load_sem.at[1]),
        pltpu.make_async_copy(ck_hbm, image.at[0, 0], load_sem.at[2]),
        pltpu.make_async_copy(cv_hbm, image.at[0, 1], load_sem.at[3]),
    ]
    other_loads = [
        pltpu.make_async_copy(bases_hbm, bases, load_sem.at[4]),
        pltpu.make_async_copy(inners_hbm, inners, load_sem.at[5]),
        pltpu.make_async_copy(q_hbm, q_in, load_sem.at[6]),
        pltpu.make_async_copy(cq_hbm, cq_in, load_sem.at[7]),
    ]
    for load in kv_loads:
        load.start()
    barrier = pltpu.get_barrier_semaphore()
    for mask in masks:
        pl.semaphore_signal(
            barrier, inc=1, device_id={"context": partner[mask]},
            device_id_type=pl.DeviceIdType.MESH)
    for load in other_loads:
        load.start()
    for load in kv_loads:
        load.wait()
    pl.semaphore_wait(barrier, len(masks))

    started = []

    def text_copy(item, part, mask):
        way = masks.index(mask)
        return pltpu.make_async_remote_copy(
            src_ref=text.at[item, part], dst_ref=text.at[item ^ mask, part],
            send_sem=text_send.at[item, part, way], recv_sem=text_recv.at[item ^ mask, part],
            device_id={"context": partner[mask]}, device_id_type=pl.DeviceIdType.MESH)

    def image_copy(item, mask):
        way = masks.index(mask)
        return pltpu.make_async_remote_copy(
            src_ref=image.at[item], dst_ref=image.at[item ^ mask],
            send_sem=image_send.at[item, way], recv_sem=image_recv.at[item ^ mask],
            device_id={"context": partner[mask]}, device_id_type=pl.DeviceIdType.MESH)

    def start(copy):
        copy.start()
        started.append(copy)

    def forward_text(item, part):
        for mask, held in text_steps:
            if item in held:
                start(text_copy(item, part, mask))

    def forward_image(item):
        for mask, held in image_steps:
            if item in held:
                start(image_copy(item, mask))

    def arrive_text(item):
        for part in range(2):
            text_copy(item ^ masks[0], part, masks[0]).wait_recv()
            forward_text(item, part)

    def arrive_image(item):
        image_copy(item ^ masks[0], masks[0]).wait_recv()
        forward_image(item)

    forward_text(0, 0)
    forward_text(0, 1)
    forward_image(0)

    for load in other_loads:
        load.wait()

    def angles(place):
        cosines, sines, starts = [], [], []
        for part in range(2):
            span = order[2 * place + part]
            base_cos = bases[0, pl.ds(span, 1), :]
            base_sin = bases[1, pl.ds(span, 1), :]
            cosines.append(base_cos * inners[0] - base_sin * inners[1])
            sines.append(base_sin * inners[2] + base_cos * inners[3])
            starts.append(span * span_len)
        return jnp.concatenate(cosines, 0), jnp.concatenate(sines, 0), starts

    def rotate(values, cosine, sine):
        values = values.astype(jnp.float32)
        turned = pltpu.roll(values, HEAD_DIM // 2, 1)
        return (values * cosine + turned * sine).astype(jnp.bfloat16)

    def positions(starts, shape, axis):
        index = lax.broadcasted_iota(jnp.int32, shape, axis)
        result = starts[0] + index
        for at in range(1, len(starts)):
            result = jnp.where(index < at * span_len, result, starts[at] + index - at * span_len)
        return result

    own_cos, own_sin, own_starts = angles(me)
    own_places = positions(own_starts, (rows, 1), 0)
    for head in range(kv_local * GROUP):
        q_rot[head // GROUP, pl.ds(head % GROUP * rows, rows), :] = rotate(
            q_in[:, head * HEAD_DIM:(head + 1) * HEAD_DIM], own_cos, own_sin)

    def dot_nt(a, b):
        return lax.dot_general(a, b, (((1,), (1,)), ((), ())), preferred_element_type=jnp.float32)

    def join(pieces):
        return pieces[0] if len(pieces) == 1 else jnp.concatenate(pieces, 0)

    def block(items, first=False, last=False):
        parts = [angles(flipped(me, item)) for item in items]
        cosine, sine = join([p[0] for p in parts]), join([p[1] for p in parts])
        width = rows * len(items)
        allowed = positions(sum([p[2] for p in parts], []), (1, width), 1) <= own_places
        for head in range(kv_local):
            columns = slice(head * HEAD_DIM, (head + 1) * HEAD_DIM)
            keys = rotate(join([text[item, 0, :, columns] for item in items]), cosine, sine)
            scores = dot_nt(q_rot[head], keys) * SCALE
            scores = jnp.where(allowed[None], scores.reshape(GROUP, rows, width), NEG_FILL)
            scores = scores.reshape(GROUP * rows, width)
            top = jnp.max(scores, -1, keepdims=True)
            if not first:
                old = peak[head]
                top = jnp.maximum(top, old)
            weights = jnp.exp2(scores - top)
            summed = jnp.sum(weights, -1, keepdims=True)
            product = jnp.dot(
                weights.astype(jnp.bfloat16), join([text[item, 1, :, columns] for item in items]),
                preferred_element_type=jnp.float32)
            if not first:
                factor = jnp.exp2(old - top)
                summed = summed + total[head] * factor
                product = product + mixed[head] * factor
            if last:
                store(out_v, head, product / summed)
            else:
                peak[head] = top
                total[head] = summed
                mixed[head] = product

    def store(target, head, result):
        result = result.astype(jnp.bfloat16)
        for g in range(GROUP):
            at = head * GROUP + g
            target[:, at * HEAD_DIM:(at + 1) * HEAD_DIM] = result[g * rows:(g + 1) * rows]

    def cross():
        keys_all = image[:, 0].astype(jnp.float32).reshape(n * image_rows, -1).astype(jnp.bfloat16)
        values_all = image[:, 1].astype(jnp.float32).reshape(n * image_rows, -1).astype(jnp.bfloat16)
        for head in range(kv_local):
            columns = slice(head * HEAD_DIM, (head + 1) * HEAD_DIM)
            queries = jnp.concatenate(
                [cq_in[:, h * HEAD_DIM:(h + 1) * HEAD_DIM] for h in range(head * GROUP, (head + 1) * GROUP)], 0)
            scores = dot_nt(queries, keys_all[:, columns]) * SCALE
            weights = jnp.exp2(scores - jnp.max(scores, -1, keepdims=True))
            summed = jnp.sum(weights, -1, keepdims=True)
            product = jnp.dot(
                weights.astype(jnp.bfloat16), values_all[:, columns], preferred_element_type=jnp.float32)
            store(cout_v, head, product / summed)

    block([0], first=True)
    if n == 8 and nx == 2:
        arrive_text(4)
        arrive_text(2)
        arrive_image(4)
        arrive_text(1)
        arrive_image(1)
        arrive_image(5)
        block([1, 2, 4])
        arrive_text(6)
        for item in (2, 3, 6, 7):
            arrive_image(item)
        arrive_text(5)
        arrive_text(3)
        block([3, 5, 6])
        cross()
        arrive_text(7)
        block([7], last=True)
    else:
        for mask, held in text_steps:
            for item in held:
                arrive_text(item ^ mask)
        for mask, held in image_steps:
            for item in held:
                arrive_image(item ^ mask)

        def step(item, unused):
            block([item])
            return 0

        lax.fori_loop(1, n, step, 0)
        for head in range(kv_local):
            store(out_v, head, mixed[head] / total[head])
        cross()
    for copy in started:
        copy.wait_send()


def body(n, nx, self_queries, self_keys, self_values, cross_queries, cross_keys, cross_values, span_order):
    rows, width = self_queries.shape
    kv_width = self_keys.shape[1]
    kv_local = kv_width // HEAD_DIM
    image_rows = cross_keys.shape[0]
    bases, inners = rotary_tables(span_order.shape[0], rows // 2)
    anywhere = pl.BlockSpec(memory_space=pl.ANY)
    ways = n.bit_length() - 1
    result = pltpu.VMEM((rows, width), jnp.bfloat16)
    return pl.pallas_call(
        functools.partial(kernel, n, nx),
        out_shape=(result, result),
        in_specs=[pl.BlockSpec(memory_space=pltpu.SMEM)] + [anywhere] * 8,
        out_specs=(pl.BlockSpec(memory_space=pltpu.VMEM),) * 2,
        scratch_shapes=[
            pltpu.VMEM((n, 2, rows, kv_width), jnp.bfloat16),
            pltpu.VMEM((n, 2, image_rows, kv_width), jnp.bfloat16),
            pltpu.VMEM((rows, width), jnp.bfloat16),
            pltpu.VMEM((rows, width), jnp.bfloat16),
            pltpu.VMEM(bases.shape, jnp.float32),
            pltpu.VMEM(inners.shape, jnp.float32),
            pltpu.VMEM((kv_local, GROUP * rows, HEAD_DIM), jnp.bfloat16),
            pltpu.VMEM((kv_local, GROUP * rows, 1), jnp.float32),
            pltpu.VMEM((kv_local, GROUP * rows, 1), jnp.float32),
            pltpu.VMEM((kv_local, GROUP * rows, HEAD_DIM), jnp.float32),
            pltpu.SemaphoreType.DMA((8,)),
            pltpu.SemaphoreType.DMA((n, 2, ways)),
            pltpu.SemaphoreType.DMA((n, 2)),
            pltpu.SemaphoreType.DMA((n, ways)),
            pltpu.SemaphoreType.DMA((n,)),
        ],
        compiler_params=pltpu.CompilerParams(collective_id=0, has_side_effects=True),
    )(span_order, self_queries, self_keys, self_values, cross_queries, cross_keys, cross_values, bases, inners)


def fast_axis(mesh, n):
    line = mesh.devices[0, :, 0]
    coords = [getattr(device, "coords", None) for device in line]
    if any(c is None for c in coords):
        return 1
    nx = len({c[0] for c in coords})
    return nx if n % nx == 0 else 1


def solution(mesh):
    n = mesh.shape["context"]
    both = P(("groups", "context"), "tensor")
    return jax.shard_map(
        functools.partial(body, n, fast_axis(mesh, n)), mesh=mesh,
        in_specs=(both,) * 6 + (P("groups"),), out_specs=(both, both), check_vma=False)
```

time: 27 us -> 23.6 us (0.87)
  Pallas kernels: 23.9 us -> 21.5 us
  local copies, waits for them, and re-layouts: 2.3 us -> 1.33 us
    pallas_call x1, Pallas kernels: 23.9 us -> 21.5 us  [body(): pl.pallas_call(functools.partial(kernel, n, nx), out_shape=(result, resul...]
    unnamed x4 -> x2, local copies, waits for them, and re-layouts: 2.3 us -> 1.33 us
where the time goes in v2:
time: 23.6 us; the launch traced here: 23.4 us
  Pallas kernels  21.5 us (91%)
  local copies, waits for them, and re-layouts  1.33 us (6%)
  between operations  0.64 us (3%)
    pallas_call x1, Pallas kernels, body(): pl.pallas_call(functools.partial(kernel, n, nx), out_shape=(result, resul...  21.5 us
    unnamed x2, local copies, waits for them, and re-layouts  1.33 us

profile of v2, /device:TPU:0, one launch (start us, length us, event | category | flops | bytes accessed | tf_op | source)
XLA Modules:
  0.0 23.4 jit_solution(15453483956307826982)
XLA Ops:
  0.6 21.5 %shard_map.104 = (bf16[80,1024]{1,0:T(8,128)(2,1)S(1)}, bf16[80,1024]{1,0:T(8,128)(2,1)S(1)}) custom-call(s32[16]{0:T(128)} %order.1, bf16[80,1024]{1,0:T(8,128)(2,1)} %q_hbm.1, bf16[80,256]{1,0:T(8,128)(2,1)} %k_hbm.1, bf16[80,256]{1,0:T(8,128)(2,1)} %v_hbm.1, bf16[80,1024]{1,0:T(8,128)(2,1)} %cq_hbm.1, bf16[24,256]{1,0:T(8,128)(2,1)} %ck_hbm.1, ...), custom_call_target="tpu_custom_call" | custom-call | tf_op jit(solution)/shard_map/pallas_call | solution.py:271
  22.1 0.7 %copy.13 = bf16[80,1024]{1,0:T(8,128)(2,1)} copy(bf16[80,1024]{1,0:T(8,128)(2,1)S(1)} %get-tuple-element.2) | data formatting | bytes 327680
  22.8 0.7 %copy.14 = bf16[80,1024]{1,0:T(8,128)(2,1)} copy(bf16[80,1024]{1,0:T(8,128)(2,1)S(1)} %get-tuple-element.3) | data formatting | bytes 327680

commit v3 on v2

--- a/solution.py
+++ b/solution.py
@@ -53,8 +53,11 @@
     x_masks = [1 << b for b in reversed(range(nx.bit_length() - 1))]
     z_masks = [nx << b for b in reversed(range((n // nx).bit_length() - 1))]
     masks = z_masks + x_masks
-    text_steps = doubling(z_masks + x_masks)
-    image_steps = doubling(z_masks[:1] + x_masks + z_masks[1:])
+    z_x = doubling(z_masks + x_masks)
+    z_x_z = doubling(z_masks[:1] + x_masks + z_masks[1:])
+    x_z = doubling(x_masks + z_masks)
+    part_steps = (z_x, z_x)
+    image_steps = x_z
 
     def flipped(index, item):
         for mask in masks:
@@ -64,6 +67,11 @@
 
     partner = {mask: flipped(me, mask) for mask in masks}
 
+    barrier = pltpu.get_barrier_semaphore()
+    for mask in masks:
+        pl.semaphore_signal(
+            barrier, inc=1, device_id={"context": partner[mask]},
+            device_id_type=pl.DeviceIdType.MESH)
     kv_loads = [
         pltpu.make_async_copy(k_hbm, text.at[0, 0], load_sem.at[0]),
         pltpu.make_async_copy(v_hbm, text.at[0, 1], load_sem.at[1]),
@@ -78,11 +86,6 @@
     ]
     for load in kv_loads:
         load.start()
-    barrier = pltpu.get_barrier_semaphore()
-    for mask in masks:
-        pl.semaphore_signal(
-            barrier, inc=1, device_id={"context": partner[mask]},
-            device_id_type=pl.DeviceIdType.MESH)
     for load in other_loads:
         load.start()
     for load in kv_loads:
@@ -110,7 +113,7 @@
         started.append(copy)
 
     def forward_text(item, part):
-        for mask, held in text_steps:
+        for mask, held in part_steps[part]:
             if item in held:
                 start(text_copy(item, part, mask))
 
@@ -119,10 +122,9 @@
             if item in held:
                 start(image_copy(item, mask))
 
-    def arrive_text(item):
-        for part in range(2):
-            text_copy(item ^ masks[0], part, masks[0]).wait_recv()
-            forward_text(item, part)
+    def arrive_text(item, part):
+        text_copy(item ^ masks[0], part, masks[0]).wait_recv()
+        forward_text(item, part)
 
     def arrive_image(item):
         image_copy(item ^ masks[0], masks[0]).wait_recv()
@@ -221,28 +223,31 @@
                 weights.astype(jnp.bfloat16), values_all[:, columns], preferred_element_type=jnp.float32)
             store(cout_v, head, product / summed)
 
+    def run_events(events):
+        for event in events.split():
+            kind, items = event[0], [int(digit) for digit in event[1:]]
+            if kind == "B":
+                block(items)
+            elif kind == "L":
+                block(items, last=True)
+            elif kind == "C":
+                cross()
+            elif kind == "i":
+                for item in items:
+                    arrive_image(item)
+            else:
+                for item in items:
+                    arrive_text(item, "KV".index(kind))
+
     block([0], first=True)
     if n == 8 and nx == 2:
-        arrive_text(4)
-        arrive_text(2)
-        arrive_image(4)
-        arrive_text(1)
-        arrive_image(1)
-        arrive_image(5)
-        block([1, 2, 4])
-        arrive_text(6)
-        for item in (2, 3, 6, 7):
-            arrive_image(item)
-        arrive_text(5)
-        arrive_text(3)
-        block([3, 5, 6])
-        cross()
-        arrive_text(7)
-        block([7], last=True)
+        run_events(
+            'K4 V4 K2 V2 K1 V1 i1 i4 B124 K6 V6 i5 K3 V3 K5 V5 B356 i2367 C K7 V7 L7')
     else:
-        for mask, held in text_steps:
-            for item in held:
-                arrive_text(item ^ mask)
+        for part in range(2):
+            for mask, held in part_steps[part]:
+                for item in held:
+                    arrive_text(item ^ mask, part)
         for mask, held in image_steps:
             for item in held:
                 arrive_image(item ^ mask)
@@ -257,6 +262,17 @@
         cross()
     for copy in started:
         copy.wait_send()
+
+
+def flush(self_v, cross_v, self_hbm, cross_hbm, sems):
+    copies = [
+        pltpu.make_async_copy(self_v, self_hbm, sems.at[0]),
+        pltpu.make_async_copy(cross_v, cross_hbm, sems.at[1]),
+    ]
+    for copy in copies:
+        copy.start()
+    for copy in copies:
+        copy.wait()
 
 
 def body(n, nx, self_queries, self_keys, self_values, cross_queries, cross_keys, cross_values, span_order):
@@ -268,7 +284,7 @@
     anywhere = pl.BlockSpec(memory_space=pl.ANY)
     ways = n.bit_length() - 1
     result = pltpu.VMEM((rows, width), jnp.bfloat16)
-    return pl.pallas_call(
+    held = pl.pallas_call(
         functools.partial(kernel, n, nx),
         out_shape=(result, result),
         in_specs=[pl.BlockSpec(memory_space=pltpu.SMEM)] + [anywhere] * 8,
@@ -292,6 +308,14 @@
         ],
         compiler_params=pltpu.CompilerParams(collective_id=0, has_side_effects=True),
     )(span_order, self_queries, self_keys, self_values, cross_queries, cross_keys, cross_values, bases, inners)
+    plain = jax.ShapeDtypeStruct((rows, width), jnp.bfloat16)
+    return pl.pallas_call(
+        flush,
+        out_shape=(plain, plain),
+        in_specs=[pl.BlockSpec(memory_space=pltpu.VMEM)] * 2,
+        out_specs=(anywhere, anywhere),
+        scratch_shapes=[pltpu.SemaphoreType.DMA((2,))],
+    )(*[pltpu.with_memory_space_constraint(array, pltpu.VMEM) for array in held])
 
 
 def fast_axis(mesh, n):

time: 23.6 us -> 21.7 us (0.919)
  local copies, waits for them, and re-layouts: 1.33 us -> 0 us
  Pallas kernels: 21.5 us -> 20.9 us
    unnamed x2 -> x0, local copies, waits for them, and re-layouts: 1.33 us -> none
    pallas_call x1, Pallas kernels: 21.5 us -> 20.2 us  [body(): pl.pallas_call(functools.partial(kernel, n, nx), out_shape=(result, resul...]
    pallas_call x0 -> x1, Pallas kernels: none -> 0.74 us  [body(): pl.pallas_call(flush, out_shape=(plain, plain), in_specs=[pl.BlockSpec(me...]
where the time goes in v3:
time: 21.7 us; the launch traced here: 21.5 us
  Pallas kernels  20.9 us (96%)
  between operations  0.64 us (3%)
    pallas_call x1, Pallas kernels, body(): pl.pallas_call(functools.partial(kernel, n, nx), out_shape=(result, resul...  20.2 us
    pallas_call x1, Pallas kernels, body(): pl.pallas_call(flush, out_shape=(plain, plain), in_specs=[pl.BlockSpec(me...  0.74 us

profile of v3, /device:TPU:0, one launch (start us, length us, event | category | flops | bytes accessed | tf_op | source)
XLA Modules:
  0.0 21.5 jit_solution(6416531945333414825)
XLA Ops:
  0.6 20.2 %shard_map.104 = (bf16[80,1024]{1,0:T(8,128)(2,1)S(1)}, bf16[80,1024]{1,0:T(8,128)(2,1)S(1)}) custom-call(s32[16]{0:T(128)} %order.1, bf16[80,1024]{1,0:T(8,128)(2,1)} %q_hbm.1, bf16[80,256]{1,0:T(8,128)(2,1)} %k_hbm.1, bf16[80,256]{1,0:T(8,128)(2,1)} %v_hbm.1, bf16[80,1024]{1,0:T(8,128)(2,1)} %cq_hbm.1, bf16[24,256]{1,0:T(8,128)(2,1)} %ck_hbm.1, ...), custom_call_target="tpu_custom_call" | custom-call | tf_op jit(solution)/shard_map/pallas_call | solution.py:287
  20.8 0.7 %shard_map.105 = (bf16[80,1024]{1,0:T(8,128)(2,1)}, bf16[80,1024]{1,0:T(8,128)(2,1)}) custom-call(bf16[80,1024]{1,0:T(8,128)(2,1)S(1)} %get-tuple-element.4.self_v, bf16[80,1024]{1,0:T(8,128)(2,1)S(1)} %get-tuple-element.5.cross_v), custom_call_target="tpu_custom_call" | custom-call | tf_op jit(solution)/shard_map/pallas_call | solution.py:312

commit v4 on v3

--- a/solution.py
+++ b/solution.py
@@ -224,7 +224,7 @@
             store(cout_v, head, product / summed)
 
     def run_events(events):
-        for event in events.split():
+        for event in events:
             kind, items = event[0], [int(digit) for digit in event[1:]]
             if kind == "B":
                 block(items)
@@ -241,8 +241,9 @@
 
     block([0], first=True)
     if n == 8 and nx == 2:
-        run_events(
-            'K4 V4 K2 V2 K1 V1 i1 i4 B124 K6 V6 i5 K3 V3 K5 V5 B356 i2367 C K7 V7 L7')
+        run_events((
+            "K4", "V4", "K2", "V2", "K1", "V1", "i1", "i4", "B124", "K6", "V6", "i5",
+            "K3", "V3", "K5", "V5", "B356", "i2367", "C", "K7", "V7", "L7"))
     else:
         for part in range(2):
             for mask, held in part_steps[part]:

time: 21.7 us -> 21.7 us (level)
  no operation moved by 1% of the time
where the time goes in v4:
time: 21.7 us; the launch traced here: 21.5 us
  Pallas kernels  20.9 us (96%)
  between operations  0.64 us (3%)
    pallas_call x1, Pallas kernels, body(): pl.pallas_call(functools.partial(kernel, n, nx), out_shape=(result, resul...  20.2 us
    pallas_call x1, Pallas kernels, body(): pl.pallas_call(flush, out_shape=(plain, plain), in_specs=[pl.BlockSpec(me...  0.74 us

profile of v4, /device:TPU:0, one launch (start us, length us, event | category | flops | bytes accessed | tf_op | source)
XLA Modules:
  0.0 21.5 jit_solution(6416531945333414825)
XLA Ops:
  0.6 20.2 %shard_map.104 = (bf16[80,1024]{1,0:T(8,128)(2,1)S(1)}, bf16[80,1024]{1,0:T(8,128)(2,1)S(1)}) custom-call(s32[16]{0:T(128)} %order.1, bf16[80,1024]{1,0:T(8,128)(2,1)} %q_hbm.1, bf16[80,256]{1,0:T(8,128)(2,1)} %k_hbm.1, bf16[80,256]{1,0:T(8,128)(2,1)} %v_hbm.1, bf16[80,1024]{1,0:T(8,128)(2,1)} %cq_hbm.1, bf16[24,256]{1,0:T(8,128)(2,1)} %ck_hbm.1, ...), custom_call_target="tpu_custom_call" | custom-call | tf_op jit(solution)/shard_map/pallas_call | solution.py:288
  20.8 0.7 %shard_map.105 = (bf16[80,1024]{1,0:T(8,128)(2,1)}, bf16[80,1024]{1,0:T(8,128)(2,1)}) custom-call(bf16[80,1024]{1,0:T(8,128)(2,1)S(1)} %get-tuple-element.4.self_v, bf16[80,1024]{1,0:T(8,128)(2,1)S(1)} %get-tuple-element.5.cross_v), custom_call_target="tpu_custom_call" | custom-call | tf_op jit(solution)/shard_map/pallas_call | solution.py:313
